TPU v7x, 32 devices: a whole 2x2x4 slice. The times are simulated.
32 devices in a mesh: owner: 16 (over z, y, core), rows: 2 (over x).
Axes of the slice: x: 2, y: 2, z: 4, core: 2. Of those that a mesh axis runs over, the one named last changes fastest.
Arguments:
- w_gate: float32 [64, 2048, 1024], P('owner', 'rows'), may hold values from -0.1875 to 0.1875
- avg_gate: float32 [64, 2048, 1024], P('owner', 'rows'), may hold values from -0.125 to 0.125
- w_up: float32 [64, 2048, 1024], P('owner', 'rows'), may hold values from -0.1875 to 0.1875
- avg_up: float32 [64, 2048, 1024], P('owner', 'rows'), may hold values from -0.125 to 0.125
- mix_share: float32 [64], P('owner'), may hold values from 0.2 to 0.8
- router_weight: float32 [2048, 64], P('rows', 'owner'), may hold values from -0.125 to 0.125
- router_gain: float32 [2048], P('rows'), may hold values from 0.25 to 1.75
Outputs:
- serve_gate: bfloat16 [64, 2048, 1024], P('owner')
- serve_up: bfloat16 [64, 2048, 1024], P('owner')
- scale_gate: float32 [64, 1024], P('owner')
- scale_up: float32 [64, 1024], P('owner')
- serve_router: bfloat16 [2048, 64], replicated
All inputs are finite; a program needn't handle non-finite values.
Results may differ from a plain program's by a relative error of at most 0.0015.
Values may be sent and summed in bfloat16 or wider, within the bound.
No kernel may reach another device: no remote copies, remote signals or barrier semaphores. Data moves between devices by JAX's collectives and lax.ppermute only.
A program may use at most 192 MiB of HBM per device.

v0:
```python
import jax
import jax.numpy as jnp
from jax import lax
from jax.sharding import PartitionSpec as P


def shards(w_gate, avg_gate, w_up, avg_up, mix_share, router_weight, router_gain):
    fresh_gate = mix_share[:, None, None] * w_gate + (1.0 - mix_share[:, None, None]) * avg_gate
    fresh_up = mix_share[:, None, None] * w_up + (1.0 - mix_share[:, None, None]) * avg_up
    total_gate, total_up = lax.psum(
        (jnp.sum(fresh_gate * fresh_gate, axis=1), jnp.sum(fresh_up * fresh_up, axis=1)), "rows"
    )
    scale_gate = jnp.sqrt(total_gate)
    scale_up = jnp.sqrt(total_up)
    narrow_gate, narrow_up = (
        (fresh_gate / jnp.expand_dims(scale_gate, 1)).astype(jnp.bfloat16),
        (fresh_up / jnp.expand_dims(scale_up, 1)).astype(jnp.bfloat16),
    )
    serve_gate, serve_up = (
        lax.all_gather(narrow_gate, "rows", axis=1, tiled=True),
        lax.all_gather(narrow_up, "rows", axis=1, tiled=True),
    )
    part_router = (router_weight * router_gain[:, None]).astype(jnp.bfloat16)
    row_router = lax.all_gather(part_router, "rows", axis=0, tiled=True)
    serve_router = lax.all_gather(row_router, "owner", axis=1, tiled=True)
    return (serve_gate, serve_up, scale_gate, scale_up, serve_router)


def solution(mesh):
    placed = (
        P("owner", "rows", None),
        P("owner", "rows", None),
        P("owner", "rows", None),
        P("owner", "rows", None),
        P("owner"),
        P("rows", "owner"),
        P("rows"),
    )
    return jax.shard_map(
        shards,
        mesh=mesh,
        in_specs=placed,
        out_specs=(
            P("owner", None, None),
            P("owner", None, None),
            P("owner", None),
            P("owner", None),
            P(),
        ),
        check_vma=False,
    )
```

profile of v0, /device:TPU:0, one launch (start us, length us, event | category | flops | bytes accessed | tf_op | source)
XLA Modules:
  0.0 499.9 jit_solution(627092504670110036)
XLA Ops:
  7.2 0.0 all-gather.4.cloned.1.call-start
  7.2 0.7 broadcast_subtract_fusion
  7.9 0.0 copy-start.5
  7.9 22.6 %multiply_reduce_fusion = (f32[4,1024]{1,0:T(4,128)S(1)}, f32[4,1024]{1,0:T(4,128)S(1)}) fusion(f32[4,1024,1024]{2,1,0:T(8,128)} %param.10, f32[4]{0:T(128)S(1)} %broadcast_subtract_fusion, f32[4,1024,1024]{2,1,0:T(8,128)} %param.9, f32[4]{0:T(128)} %param.11, f32[4,1024,1024]{2,1,0:T(8,128)} %param.8, f32[4,1024,1024]{2,1,0:T(8,128)} %param.7), kind=kLoop, calls=%fused_computation.1 | loop fusion | flops 41934848 | bytes 67141664 | tf_op jit(solution)/shard_map/reduce_sum | solution.py:11
  30.5 9.9 %all-reduce = (f32[4,1024]{1,0:T(4,128)S(1)}, f32[4,1024]{1,0:T(4,128)S(1)}) all-reduce(f32[4,1024]{1,0:T(4,128)S(1)} %get-tuple-element.6, f32[4,1024]{1,0:T(4,128)S(1)} %get-tuple-element.5), channel_id=1, replica_groups=mesh['owner'=16,'rows'=2] {'rows'}, use_global_device_ids=true, to_apply=%region_1.0 | all-reduce | flops 8192 | bytes 65536 | tf_op jit(solution)/shard_map/psum | solution.py:10
  40.5 0.0 copy-start.1
  40.5 0.0 copy-done.5
  40.5 0.0 copy-start.2
  40.5 29.3 %divide_convert_fusion = (bf16[4,1024,1024]{2,1,0:T(8,128)(2,1)}, bf16[4,1024,1024]{2,1,0:T(8,128)(2,1)}) fusion(f32[4,1024]{1,0:T(4,128)S(1)} %sqrt.7, f32[4,1024,1024]{2,1,0:T(8,128)} %param.10, f32[4]{0:T(128)S(1)} %broadcast_subtract_fusion, f32[4,1024,1024]{2,1,0:T(8,128)} %param.9, f32[4]{0:T(128)S(1)} %copy-done.5, f32[4,1024]{1,0:T(4,128)S(1)} %sqrt.6, ...), kind=kLoop, calls=%fused_computation | loop fusion | flops 41943040 | bytes 83918880 | tf_op jit(solution)/shard_map/convert_element_type | solution.py:17
  69.8 0.0 copy-done.1
  69.8 0.0 copy-done.2
  69.8 0.0 copy-start.3
  69.9 0.0 copy-start.4
  69.9 0.0 all-gather.4.cloned.1.call-update
  69.9 0.0 all-gather.6.cloned.1.call-start
  69.9 0.7 all-gather.6.cloned.1.call-update
  70.6 0.0 copy-done.3
  70.7 0.0 copy-done.4
  70.7 4.4 all_gather.14
  75.0 22.2 %all-gather = bf16[16,4,2048]{2,1,0:T(4,128)(2,1)S(1)} all-gather(bf16[1,4,2048]{2,1,0:T(4,128)(2,1)S(1)} %bitcast.5), channel_id=1, replica_groups=mesh['owner'=16,'rows'=2] {'owner'}, dimensions={0}, use_global_device_ids=true | all-gather | bytes 278528 | tf_op jit(solution)/shard_map/all_gather | solution.py:25
  97.3 0.8 reshape.17
  98.0 171.1 %all-gather.4.cloned.1.call-done = bf16[4,2048,1024]{2,1,0:T(8,128)(2,1)} async-done(((bf16[4,1024,1024]{2,1,0:T(8,128)(2,1)}), bf16[4,2048,1024]{2,1,0:T(8,128)(2,1)}) %all-gather.4.cloned.1.call-update) | async-done | bytes 16777232 | tf_op jit(solution)/shard_map/all_gather | solution.py:20
  269.1 201.0 %all-gather.6.cloned.1.call-done = bf16[4,2048,1024]{2,1,0:T(8,128)(2,1)} async-done(((bf16[4,1024,1024]{2,1,0:T(8,128)(2,1)}), bf16[4,2048,1024]{2,1,0:T(8,128)(2,1)}) %all-gather.6.cloned.1.call-update) | async-done | bytes 16777232 | tf_op jit(solution)/shard_map/all_gather | solution.py:21
  470.1 0.0 copy-start
  470.1 14.8 %copy.14 = bf16[4,2048,1024]{2,1,0:T(8,128)(2,1)} copy(bf16[4,2048,1024]{2,1,0:T(8,128)(2,1)} %all-gather.4.cloned.1.call-done) | data formatting | bytes 33554432
  484.8 2.1 copy-done
  486.9 6.2 %copy.15 = bf16[4,2048,1024]{2,1,0:T(8,128)(2,1)} copy(bf16[4,2048,1024]{2,1,0:T(8,128)(2,1)S(1)} %copy-done) | data formatting | bytes 33554432
  (3 shorter events, 0.0 us)
Async XLA Ops:
  7.2 261.9 %all-gather.4.cloned.1.call-start = ((), (), s32[]{:S(2)}) async-start(), calls=%async_computation | async-start | bytes 25165824 | tf_op jit(solution)/shard_map/all_gather | solution.py:20
  7.9 32.6 %copy-start.5 = (f32[4]{0:T(128)S(1)}, f32[4]{0:T(128)}, u32[]{:S(2)}) copy-start(f32[4]{0:T(128)} %param.11) | copy-start | bytes 52
  40.5 29.4 %copy-start.1 = (f32[4,1024]{1,0:T(4,128)}, f32[4,1024]{1,0:T(4,128)S(1)}, u32[]{:S(2)}) copy-start(f32[4,1024]{1,0:T(4,128)S(1)} %sqrt.6) | copy-start | bytes 49156
  40.5 29.3 %copy-start.2 = (f32[4,1024]{1,0:T(4,128)}, f32[4,1024]{1,0:T(4,128)S(1)}, u32[]{:S(2)}) copy-start(f32[4,1024]{1,0:T(4,128)S(1)} %sqrt.7) | copy-start | bytes 49156
  69.8 0.8 copy-start.3
  69.9 0.8 copy-start.4
  69.9 400.2 %all-gather.6.cloned.1.call-start = ((), (), s32[]{:S(2)}) async-start(), calls=%async_computation.1 | async-start | bytes 25165824 | tf_op jit(solution)/shard_map/all_gather | solution.py:21
  470.1 16.9 %copy-start = (bf16[4,2048,1024]{2,1,0:T(8,128)(2,1)S(1)}, bf16[4,2048,1024]{2,1,0:T(8,128)(2,1)}, u32[]{:S(2)}) copy-start(bf16[4,2048,1024]{2,1,0:T(8,128)(2,1)} %all-gather.6.cloned.1.call-done) | copy-start | bytes 50331652
Sparse Core Ops, SparseCore 0:
  70.0 199.0 all-gather.3
  271.2 198.8 all-gather.5
where the time goes:
time: 500 us
  waiting for transfers between devices  373 us (75%)
  other arithmetic  52.6 us (11%)
  blocking collectives  36.5 us (7%)
  local copies, waits for them, and re-layouts  23.9 us (5%)
  between operations  14.1 us (3%)
    all_gather x1, waiting for transfers between devices, shards(): lax.all_gather(narrow_up, 'rows', axis=1, tiled=True)  201 us
    all_gather x1, waiting for transfers between devices, shards(): lax.all_gather(narrow_gate, 'rows', axis=1, tiled=True)  171 us
    convert_element_type x1, other arithmetic, shards(): (fresh_up / jnp.expand_dims(scale_up, 1)).astype(jnp.bfloat16)  29.3 us
    unnamed x15, local copies, waits for them, and re-layouts  23.8 us
    reduce_sum x1, other arithmetic, shards(): jnp.sum(fresh_up * fresh_up, axis=1)  22.6 us
    all_gather x1, blocking collectives, shards(): serve_router = lax.all_gather(row_router, 'owner', axis=1, tiled=True)  22.2 us
  transfers between devices with their start and end apart: 2, of which 2 were waited for; matrix products, arithmetic and copies ran while one was open for 0% of the time, Pallas kernels for 0%

commit v1 on v0

v1 whole, which is shorter than its diff:
```python
import jax
import jax.numpy as jnp
from jax import lax
from jax.experimental import pallas as pl
from jax.experimental.pallas import tpu as pltpu
from jax.sharding import PartitionSpec as P


ANY = pl.BlockSpec(memory_space=pl.ANY)
SMALL = pl.BlockSpec(memory_space=pltpu.SMEM)


def block_rows(rows, most):
    block = min(rows, most)
    while rows % block:
        block -= 16
    return block


def column_sums(w, avg, mix, first, count, most, out, at, slots, after):
    _, rows, cols = w.shape
    block = block_rows(rows, most)
    steps = rows // block

    def kernel(mix_ref, w_ref, avg_ref, *rest):
        out_ref, acc = rest[-2], rest[-1]
        e, i = pl.program_id(0), pl.program_id(1)
        share = mix_ref[first + e]
        fresh = share * w_ref[0] + (1.0 - share) * avg_ref[0]
        part = jnp.sum((fresh * fresh).reshape(block // 8, 8, cols), axis=0)

        @pl.when(i == 0)
        def _():
            acc[...] = part

        @pl.when(i > 0)
        def _():
            acc[...] += part

        @pl.when(i == steps - 1)
        def _():
            out_ref[0] = jnp.sum(acc[...], axis=0, keepdims=True)

    spec = pl.BlockSpec((1, block, cols), lambda e, i: (first + e, i, 0))
    extra = ([] if out is None else [out]) + list(after)
    return pl.pallas_call(
        kernel,
        grid=(count, steps),
        in_specs=[SMALL, spec, spec] + [ANY] * len(extra),
        out_specs=pl.BlockSpec((1, 1, cols), lambda e, i: (at + e, 0, 0)),
        out_shape=jax.ShapeDtypeStruct((slots, 1, cols), jnp.float32),
        scratch_shapes=[pltpu.VMEM((8, cols), jnp.float32)],
        input_output_aliases={} if out is None else {3: 0},
    )(mix, w, avg, *extra)


def settle(w, avg, mix, parts, at, expert, start, count, most, place, out, whole_rows, after):
    experts, _, cols = w.shape
    block = block_rows(count, most)
    own = w.shape[1] // block

    def kernel(place_ref, mix_ref, w_ref, avg_ref, *rest):
        total = rest[0][0]
        for part_ref in rest[1 : len(parts)]:
            total = total + part_ref[0]
        send_ref, out_ref = rest[-2], rest[-1]
        share = mix_ref[expert]
        fresh = share * w_ref[0] + (1.0 - share) * avg_ref[0]
        inverse = 1.0 / jnp.sqrt(total)
        done = (fresh * inverse).astype(jnp.bfloat16)
        send_ref[0] = done
        out_ref[0] = done

    spec = pl.BlockSpec((1, block, cols), lambda i, p: (expert, start // block + i, 0))
    extra = ([] if out is None else [out]) + list(after)
    return pl.pallas_call(
        kernel,
        grid_spec=pltpu.PrefetchScalarGridSpec(
            num_scalar_prefetch=1,
            grid=(count // block,),
            in_specs=[SMALL, spec, spec]
            + [pl.BlockSpec((1, 1, cols), lambda i, p: (at, 0, 0))] * len(parts)
            + [ANY] * len(extra),
            out_specs=[
                pl.BlockSpec((1, block, cols), lambda i, p: (0, i, 0)),
                pl.BlockSpec((1, block, cols), lambda i, p: (expert, p[0] * own + start // block + i, 0)),
            ],
        ),
        out_shape=[
            pltpu.HBM((1, count, cols), jnp.bfloat16),
            pltpu.HBM((experts, whole_rows, cols), jnp.bfloat16),
        ],
        input_output_aliases={} if out is None else {4 + len(parts): 1},
    )(place, mix, w, avg, *parts, *extra)


def put(piece, source, out, expert, start, rows, most, after):
    _, count, cols = piece.shape
    block = block_rows(count, most)
    own = rows // block

    def kernel(source_ref, piece_ref, *rest):
        rest[-1][...] = piece_ref[...]

    return pl.pallas_call(
        kernel,
        grid_spec=pltpu.PrefetchScalarGridSpec(
            num_scalar_prefetch=1,
            grid=(count // block,),
            in_specs=[pl.BlockSpec((1, block, cols), lambda i, s: (0, i, 0))] + [ANY] * (1 + len(after)),
            out_specs=pl.BlockSpec((1, block, cols), lambda i, s: (expert, s[0] * own + start // block + i, 0)),
        ),
        out_shape=pltpu.HBM(out.shape, out.dtype),
        input_output_aliases={2: 0},
    )(source, piece, out, *after)


def plan(experts, rows):
    half = rows // 2
    pieces = [(0, 0, 0, half), (0, 0, half, half)]
    pieces += [(0, e, 0, rows) for e in range(1, experts)]
    pieces += [(1, e, 0, rows) for e in range(experts - 1)]
    last = (1, experts - 1)
    pieces += [(*last, 0, half), (*last, half, half // 2)]
    pieces += [(*last, half + half // 2, half // 4), (*last, half + half // 2 + half // 4, half // 4)]
    return pieces


def solution(mesh):
    ranks = mesh.shape["rows"]

    def moved(array, shift):
        return lax.ppermute(array, "rows", [(i, (i + shift) % ranks) for i in range(ranks)])

    def summands(part):
        if ranks == 2:
            return (part, moved(part, 1))
        return (jnp.sum(lax.all_gather(part, "rows"), axis=0),)

    def shards(w_gate, avg_gate, w_up, avg_up, mix_share, router_weight, router_gain):
        experts, rows, _ = w_gate.shape
        arrays = ((w_gate, avg_gate), (w_up, avg_up))
        here = lax.axis_index("rows").astype(jnp.int32).reshape(1)
        pieces = plan(experts, rows)
        outs = [None, None]
        sends = []

        part = column_sums(*arrays[0], mix_share, 0, 1, 128, None, 0, 1, ())
        first_parts = summands(part)

        def settled(k, after):
            which, expert, start, count = pieces[k]
            if which == 0 and expert == 0:
                parts, at = first_parts, 0
            else:
                parts, at = rest_parts, which * experts + expert - 1
            send, outs[which] = settle(
                *arrays[which], mix_share, parts, at, expert, start, count, 128 if k == 0 else 256,
                here, outs[which], rows * ranks, after,
            )
            sends.append(send)

        settled(0, ())
        part, slots = None, 2 * experts - 1
        if experts > 1:
            part = column_sums(*arrays[0], mix_share, 1, experts - 1, 256, None, 0, slots, (sends[0],))
        part = column_sums(*arrays[1], mix_share, 0, experts, 256, part, experts - 1, slots, (sends[0],))
        rest_parts = summands(part)

        gain, _ = lax.optimization_barrier((router_gain, part))
        part_router = (router_weight * gain[:, None]).astype(jnp.bfloat16).T
        if ranks == 2:
            other = moved(part_router, 1)
            first = here[0] == 0
            row_router = jnp.concatenate(
                [jnp.where(first, part_router, other), jnp.where(first, other, part_router)], axis=1
            )
        else:
            row_router = lax.all_gather(part_router, "rows", axis=1, tiled=True)

        for k in range(1, len(pieces)):
            settled(k, (sends[-1],) if k > 1 else (part,))

        row_router, _ = lax.optimization_barrier((row_router, sends[-1]))
        serve_router = lax.all_gather(row_router, "owner", axis=0, tiled=True).T

        after = (sends[-1],)
        for k, (which, expert, start, count) in enumerate(pieces):
            for shift in range(1, ranks):
                got = moved(sends[k], shift)
                source = (here + ranks - shift) % ranks
                outs[which] = put(got, source, outs[which], expert, start, rows, 512, after)
                after = (outs[0],) if which == 0 and pieces[(k + 1) % len(pieces)][0] == 1 else ()

        total = jnp.concatenate([sum(first_parts[1:], first_parts[0]), sum(rest_parts[1:], rest_parts[0])], axis=0)
        scales = jnp.sqrt(total[:, 0])
        scale_gate, scale_up = scales[:experts], scales[experts:]
        return (outs[0], outs[1], scale_gate, scale_up, serve_router)

    return jax.shard_map(
        shards,
        mesh=mesh,
        in_specs=(
            P("owner", "rows", None),
            P("owner", "rows", None),
            P("owner", "rows", None),
            P("owner", "rows", None),
            P("owner"),
            P("rows", "owner"),
            P("rows"),
        ),
        out_specs=(
            P("owner", None, None),
            P("owner", None, None),
            P("owner", None),
            P("owner", None),
            P(),
        ),
        check_vma=False,
    )
```

time: 500 us -> 425 us (0.85)
  Pallas kernels: 0 us -> 119 us
  waiting for transfers between devices: 373 us -> 260 us
  other arithmetic: 52.6 us -> 0.15 us
  local copies, waits for them, and re-layouts: 23.9 us -> 5.8 us
  starting transfers between devices: 0.08 us -> 15.6 us
  blocking collectives: 36.5 us -> 22.6 us
  between operations: 14.1 us -> 0.74 us
    all_gather x2 -> x0, waiting for transfers between devices: 372 us -> none  [the longest x1 201 us: shards(): lax.all_gather(narrow_up, 'rows', axis=1, tiled=True)]
    ppermute x0 -> x15, waiting for transfers between devices: none -> 260 us  [moved(): lax.ppermute(array, 'rows', [(i, (i + shift) % ranks) for i in range(rank...]
    pallas_call x0 -> x27, Pallas kernels: none -> 119 us  [the longest x12 53.6 us: settle(): pl.pallas_call(kernel, grid_spec=pltpu.PrefetchScalarGridSpec(num_scalar_...]
    convert_element_type x2 -> x0, other arithmetic: 29.3 us -> none  [the longest x1 29.3 us: shards(): (fresh_up / jnp.expand_dims(scale_up, 1)).astype(jnp.bfloat16)]
    reduce_sum x1 -> x0, other arithmetic: 22.6 us -> none  [shards(): jnp.sum(fresh_up * fresh_up, axis=1)]
    unnamed x15 -> x34, local copies, waits for them, and re-layouts: 23.8 us -> 5.8 us
    ppermute x0 -> x15, starting transfers between devices: none -> 15.6 us  [moved(): lax.ppermute(array, 'rows', [(i, (i + shift) % ranks) for i in range(rank...]
    psum x1 -> x0, blocking collectives: 9.94 us -> none  [shards(): lax.psum((jnp.sum(fresh_gate * fresh_gate, axis=1), jnp.sum(fresh_up * fr...]
  transfers between devices with their start and end apart: 2 -> 15, of which waited for: 2 -> 10; matrix products, arithmetic and copies ran while one was open for 0% -> 0% of each run, Pallas kernels for 0% -> 16%
where the time goes in v1:
time: 425 us; the launch traced here: 424 us
  waiting for transfers between devices  260 us (61%)
  Pallas kernels  119 us (28%)
  blocking collectives  22.6 us (5%)
  starting transfers between devices  15.6 us (4%)
  local copies, waits for them, and re-layouts  5.8 us (1%)
    ppermute x15, waiting for transfers between devices, moved(): lax.ppermute(array, 'rows', [(i, (i + shift) % ranks) for i in range(rank...  260 us
    pallas_call x12, Pallas kernels, settle(): pl.pallas_call(kernel, grid_spec=pltpu.PrefetchScalarGridSpec(num_scalar_...  53.6 us
    pallas_call x3, Pallas kernels, column_sums(): pl.pallas_call(kernel, grid=(count, steps), in_specs=[SMALL, spec, spec]...  37.6 us
    pallas_call x12, Pallas kernels, put(): pl.pallas_call(kernel, grid_spec=pltpu.PrefetchScalarGridSpec(num_scalar_...  27.6 us
    all_gather x1, blocking collectives, shards(): serve_router = lax.all_gather(row_router, 'owner', axis=0, tiled=True).T  22.6 us
    ppermute x15, starting transfers between devices, moved(): lax.ppermute(array, 'rows', [(i, (i + shift) % ranks) for i in range(rank...  15.6 us
  transfers between devices with their start and end apart: 15, of which 10 were waited for; matrix products, arithmetic and copies ran while one was open for 0% of the time, Pallas kernels for 16%

profile of v1, /device:TPU:0, one launch (start us, length us, event | category | flops | bytes accessed | tf_op | source)
XLA Modules:
  0.0 423.7 jit_solution(16376712077651872511)
XLA Ops:
  0.6 6.7 %shard_map.110.rest_0_ = f32[1,1,1024]{2,1,0:T(1,128)} custom-call(f32[4]{0:T(128)} %mix_ref.29, f32[4,1024,1024]{2,1,0:T(8,128)} %w_ref.22, f32[4,1024,1024]{2,1,0:T(8,128)} %avg_ref.22), custom_call_target="tpu_custom_call" | custom-call | tf_op jit(solution)/shard_map/pallas_call | solution.py:46
  7.4 3.0 collective-permute-start
  12.7 4.4 %shard_map.111 = (bf16[1,512,1024]{2,1,0:T(8,128)(2,1)}, bf16[4,2048,1024]{2,1,0:T(8,128)(2,1)}) custom-call(s32[1]{0:T(128)} %bitcast.place_ref, f32[4]{0:T(128)} %mix_ref.29, f32[4,1024,1024]{2,1,0:T(8,128)} %w_ref.22, f32[4,1024,1024]{2,1,0:T(8,128)} %avg_ref.22, f32[1,1,1024]{2,1,0:T(1,128)} %shard_map.110.rest_0_, f32[1,1,1024]{2,1,0:T(1,128)} %copy-done.13), custom_call_target="tpu_custom_call" | custom-call | tf_op jit(solution)/shard_map/pallas_call | solution.py:76
  17.1 13.4 %shard_map.112.rest_0_ = f32[7,1,1024]{2,1,0:T(1,128)} custom-call(f32[4]{0:T(128)} %mix_ref.29, f32[4,1024,1024]{2,1,0:T(8,128)} %w_ref.22, f32[4,1024,1024]{2,1,0:T(8,128)} %avg_ref.22, bf16[1,512,1024]{2,1,0:T(8,128)(2,1)} %get-tuple-element.31.rest_0_.rest_1_), custom_call_target="tpu_custom_call" | custom-call | tf_op jit(solution)/shard_map/pallas_call | solution.py:46
  30.5 17.5 %shard_map.113.rest_3_.rest_0_ = f32[7,1,1024]{2,1,0:T(1,128)} custom-call(f32[4]{0:T(128)} %mix_ref.29, f32[4,1024,1024]{2,1,0:T(8,128)} %w_ref.29, f32[4,1024,1024]{2,1,0:T(8,128)} %avg_ref.29, f32[7,1,1024]{2,1,0:T(1,128)} %shard_map.112.rest_0_, bf16[1,512,1024]{2,1,0:T(8,128)(2,1)} %get-tuple-element.31.rest_0_.rest_1_), custom_call_target="tpu_custom_call", output_to_operand_aliasing={{}: (3, {})} | custom-call | tf_op jit(solution)/shard_map/pallas_call | solution.py:46
  50.0 3.4 shard_map.114
  54.0 6.0 %shard_map.115 = (bf16[1,1024,1024]{2,1,0:T(8,128)(2,1)}, bf16[4,2048,1024]{2,1,0:T(8,128)(2,1)}) custom-call(s32[1]{0:T(128)} %bitcast.place_ref, f32[4]{0:T(128)} %mix_ref.29, f32[4,1024,1024]{2,1,0:T(8,128)} %w_ref.22, f32[4,1024,1024]{2,1,0:T(8,128)} %avg_ref.22, f32[7,1,1024]{2,1,0:T(1,128)} %shard_map.113.rest_3_.rest_0_, ...), custom_call_target="tpu_custom_call", output_to_operand_aliasing={{1}: (6, {})} | custom-call | tf_op jit(solution)/shard_map/pallas_call | solution.py:76
  62.7 5.9 %shard_map.116 = (bf16[1,1024,1024]{2,1,0:T(8,128)(2,1)}, bf16[4,2048,1024]{2,1,0:T(8,128)(2,1)}) custom-call(s32[1]{0:T(128)} %bitcast.place_ref, f32[4]{0:T(128)} %mix_ref.29, f32[4,1024,1024]{2,1,0:T(8,128)} %w_ref.22, f32[4,1024,1024]{2,1,0:T(8,128)} %avg_ref.22, f32[7,1,1024]{2,1,0:T(1,128)} %shard_map.113.rest_3_.rest_0_, ...), custom_call_target="tpu_custom_call", output_to_operand_aliasing={{1}: (6, {})} | custom-call | tf_op jit(solution)/shard_map/pallas_call | solution.py:76
  70.7 5.9 %shard_map.117 = (bf16[1,1024,1024]{2,1,0:T(8,128)(2,1)}, bf16[4,2048,1024]{2,1,0:T(8,128)(2,1)}) custom-call(s32[1]{0:T(128)} %bitcast.place_ref, f32[4]{0:T(128)} %mix_ref.29, f32[4,1024,1024]{2,1,0:T(8,128)} %w_ref.22, f32[4,1024,1024]{2,1,0:T(8,128)} %avg_ref.22, f32[7,1,1024]{2,1,0:T(1,128)} %shard_map.113.rest_3_.rest_0_, ...), custom_call_target="tpu_custom_call", output_to_operand_aliasing={{1}: (6, {})} | custom-call | tf_op jit(solution)/shard_map/pallas_call | solution.py:76
  76.6 119.6 %collective-permute-done.14 = bf16[4,1024]{1,0:T(4,128)(2,1)S(1)} collective-permute-done((bf16[4,1024]{1,0:T(4,128)(2,1)S(1)}, bf16[4,1024]{1,0:T(4,128)(2,1)S(1)}, u32[]{:S(2)}, u32[]{:S(2)}) %collective-permute-start.14) | collective-permute-done | bytes 8224 | tf_op jit(solution)/shard_map/ppermute | solution.py:133
  196.5 5.9 %shard_map.118 = (bf16[1,1024,1024]{2,1,0:T(8,128)(2,1)}, bf16[4,2048,1024]{2,1,0:T(8,128)(2,1)}) custom-call(s32[1]{0:T(128)} %bitcast.place_ref, f32[4]{0:T(128)} %mix_ref.29, f32[4,1024,1024]{2,1,0:T(8,128)} %w_ref.29, f32[4,1024,1024]{2,1,0:T(8,128)} %avg_ref.29, f32[7,1,1024]{2,1,0:T(1,128)} %shard_map.113.rest_3_.rest_0_, f32[7,1,1024]{2,1,0:T(1,128)} %copy-done.2, ...), custom_call_target="tpu_custom_call" | custom-call | tf_op jit(solution)/shard_map/pallas_call | solution.py:76
  202.4 5.9 %shard_map.119 = (bf16[1,1024,1024]{2,1,0:T(8,128)(2,1)}, bf16[4,2048,1024]{2,1,0:T(8,128)(2,1)}) custom-call(s32[1]{0:T(128)} %bitcast.place_ref, f32[4]{0:T(128)} %mix_ref.29, f32[4,1024,1024]{2,1,0:T(8,128)} %w_ref.29, f32[4,1024,1024]{2,1,0:T(8,128)} %avg_ref.29, f32[7,1,1024]{2,1,0:T(1,128)} %shard_map.113.rest_3_.rest_0_, ...), custom_call_target="tpu_custom_call", output_to_operand_aliasing={{1}: (6, {})} | custom-call | tf_op jit(solution)/shard_map/pallas_call | solution.py:76
  210.4 5.9 %shard_map.120 = (bf16[1,1024,1024]{2,1,0:T(8,128)(2,1)}, bf16[4,2048,1024]{2,1,0:T(8,128)(2,1)}) custom-call(s32[1]{0:T(128)} %bitcast.place_ref, f32[4]{0:T(128)} %mix_ref.29, f32[4,1024,1024]{2,1,0:T(8,128)} %w_ref.29, f32[4,1024,1024]{2,1,0:T(8,128)} %avg_ref.29, f32[7,1,1024]{2,1,0:T(1,128)} %shard_map.113.rest_3_.rest_0_, ...), custom_call_target="tpu_custom_call", output_to_operand_aliasing={{1}: (6, {})} | custom-call | tf_op jit(solution)/shard_map/pallas_call | solution.py:76
  218.1 3.4 shard_map.121
  222.2 2.7 shard_map.122
  229.3 15.7 %collective-permute-done.2.piece_ref = bf16[1,1024,1024]{2,1,0:T(8,128)(2,1)} collective-permute-done((bf16[1,1024,1024]{2,1,0:T(8,128)(2,1)}, bf16[1,1024,1024]{2,1,0:T(8,128)(2,1)}, u32[]{:S(2)}, u32[]{:S(2)}) %collective-permute-start.2) | collective-permute-done | bytes 2097184 | tf_op jit(solution)/shard_map/ppermute | solution.py:133
  245.3 44.6 %collective-permute-done.13.piece_ref = bf16[1,1024,1024]{2,1,0:T(8,128)(2,1)} collective-permute-done((bf16[1,1024,1024]{2,1,0:T(8,128)(2,1)}, bf16[1,1024,1024]{2,1,0:T(8,128)(2,1)}, u32[]{:S(2)}, u32[]{:S(2)}) %collective-permute-start.13) | collective-permute-done | bytes 2097184 | tf_op jit(solution)/shard_map/ppermute | solution.py:133
  290.3 44.6 %collective-permute-done.12.piece_ref = bf16[1,1024,1024]{2,1,0:T(8,128)(2,1)} collective-permute-done((bf16[1,1024,1024]{2,1,0:T(8,128)(2,1)}, bf16[1,1024,1024]{2,1,0:T(8,128)(2,1)}, u32[]{:S(2)}, u32[]{:S(2)}) %collective-permute-start.12) | collective-permute-done | bytes 2097184 | tf_op jit(solution)/shard_map/ppermute | solution.py:133
  335.2 22.6 %all-gather = bf16[16,4,2048]{2,1,0:T(4,128)(2,1)S(1)} all-gather(bf16[1,4,2048]{2,1,0:T(4,128)(2,1)S(1)} %bitcast.12), channel_id=1, replica_groups=mesh['owner'=16,'rows'=2] {'owner'}, dimensions={0}, use_global_device_ids=true | all-gather | bytes 278528 | tf_op jit(solution)/shard_map/all_gather | solution.py:185
  359.1 2.3 shard_map.125.rest_0_
  361.4 2.3 shard_map.126.rest_0_
  363.7 2.6 shard_map.127.rest_0_
  366.3 2.6 shard_map.128.rest_0_
  368.9 2.6 shard_map.129.rest_1_
  371.5 2.6 shard_map.130.rest_0_
  374.1 2.6 shard_map.131.rest_0_
  376.7 3.1 collective-permute-done.11.piece_ref
  379.8 2.6 shard_map.132.rest_0_
  382.4 19.8 %collective-permute-done.10.piece_ref = bf16[1,512,1024]{2,1,0:T(8,128)(2,1)S(1)} collective-permute-done((bf16[1,512,1024]{2,1,0:T(8,128)(2,1)}, bf16[1,512,1024]{2,1,0:T(8,128)(2,1)S(1)}, u32[]{:S(2)}, u32[]{:S(2)}) %collective-permute-start.10) | collective-permute-done | bytes 1048608 | tf_op jit(solution)/shard_map/ppermute | solution.py:133
  403.2 2.3 shard_map.133.rest_0_
  405.5 8.0 %collective-permute-done.9.piece_ref = bf16[1,256,1024]{2,1,0:T(8,128)(2,1)S(1)} collective-permute-done((bf16[1,256,1024]{2,1,0:T(8,128)(2,1)S(1)}, bf16[1,256,1024]{2,1,0:T(8,128)(2,1)S(1)}, u32[]{:S(2)}, u32[]{:S(2)}) %collective-permute-start.9) | collective-permute-done | bytes 524320 | tf_op jit(solution)/shard_map/ppermute | solution.py:133
  416.1 2.4 collective-permute-done.8.piece_ref
  (67 shorter events, 30.3 us)
Async XLA Ops:
  7.4 4.8 %collective-permute-start = (f32[1,1,1024]{2,1,0:T(1,128)}, f32[1,1,1024]{2,1,0:T(1,128)S(1)}, u32[]{:S(2)}, u32[]{:S(2)}) collective-permute-start(f32[1,1,1024]{2,1,0:T(1,128)} %shard_map.110.rest_0_), channel_id=1, source_target_pairs={{0,1},{1,0},{2,3},{3,2},{4,5},{5,4},{6,7},{7,6},{8,9},{9,8},{10,11... | collective-permute-start | bytes 12296 | tf_op jit(solution)/shard_map/ppermute | solution.py:133
  12.1 0.6 copy-start.13
  48.0 5.4 %collective-permute-start.1 = (f32[7,1,1024]{2,1,0:T(1,128)}, f32[7,1,1024]{2,1,0:T(1,128)S(1)}, u32[]{:S(2)}, u32[]{:S(2)}) collective-permute-start(f32[7,1,1024]{2,1,0:T(1,128)} %shard_map.113.rest_3_.rest_0_), channel_id=1, source_target_pairs={{0,1},{1,0},{2,3},{3,2},{4,5},{5,4},{6,7},{7,6},{8,9},{9,8},{10,11... | collective-permute-start | bytes 86024 | tf_op jit(solution)/shard_map/ppermute | solution.py:133
  53.4 0.6 copy-start.2
  54.0 6.7 %copy-start.1 = (bf16[1,512,1024]{2,1,0:T(8,128)(2,1)S(1)}, bf16[1,512,1024]{2,1,0:T(8,128)(2,1)}, u32[]{:S(2)}) copy-start(bf16[1,512,1024]{2,1,0:T(8,128)(2,1)} %get-tuple-element.31.rest_0_.rest_1_) | copy-start | bytes 3145732
  60.0 156.3 %collective-permute-start.4 = (bf16[1,1024,1024]{2,1,0:T(8,128)(2,1)}, bf16[1,1024,1024]{2,1,0:T(8,128)(2,1)S(1)}, u32[]{:S(2)}, u32[]{:S(2)}) collective-permute-start(bf16[1,1024,1024]{2,1,0:T(8,128)(2,1)} %get-tuple-element.36.rest_3_), channel_id=1, source_target_pairs={{0,1},{1,0},{2,3},{3,2},{4,5},{5,4},{6,7},{7,6},{8,9},{9,8},{10,11... | collective-permute-start | bytes 6291464 | tf_op jit(solution)/shard_map/ppermute | solution.py:133
  60.7 147.6 %collective-permute-start.6 = (bf16[1,512,1024]{2,1,0:T(8,128)(2,1)S(1)}, bf16[1,512,1024]{2,1,0:T(8,128)(2,1)}, u32[]{:S(2)}, u32[]{:S(2)}) collective-permute-start(bf16[1,512,1024]{2,1,0:T(8,128)(2,1)S(1)} %copy-done.1), channel_id=1, source_target_pairs={{0,1},{1,0},{2,3},{3,2},{4,5},{5,4},{6,7},{7,6},{8,9},{9,8},{10,11... | collective-permute-start | bytes 3145736 | tf_op jit(solution)/shard_map/ppermute | solution.py:133
  62.0 148.1 %collective-permute-start.5 = (bf16[1,512,1024]{2,1,0:T(8,128)(2,1)}, bf16[1,512,1024]{2,1,0:T(8,128)(2,1)}, u32[]{:S(2)}, u32[]{:S(2)}) collective-permute-start(bf16[1,512,1024]{2,1,0:T(8,128)(2,1)} %get-tuple-element.34.rest_3_), channel_id=1, source_target_pairs={{0,1},{1,0},{2,3},{3,2},{4,5},{5,4},{6,7},{7,6},{8,9},{9,8},{10,11... | collective-permute-start | bytes 3145736 | tf_op jit(solution)/shard_map/ppermute | solution.py:133
  62.7 7.2 %copy-start.12 = (f32[1024,4]{0,1:T(4,128)S(1)}, f32[1024,4]{0,1:T(4,128)}, u32[]{:S(2)}) copy-start(f32[1024,4]{0,1:T(4,128)} %param.12) | copy-start | bytes 49156
  62.7 7.2 %copy-start.15 = (f32[1024]{0:T(1024)S(1)}, f32[1024]{0:T(1024)}, u32[]{:S(2)}) copy-start(f32[1024]{0:T(1024)} %param.13) | copy-start | bytes 12292
  68.6 152.9 %collective-permute-start.3 = (bf16[1,1024,1024]{2,1,0:T(8,128)(2,1)}, bf16[1,1024,1024]{2,1,0:T(8,128)(2,1)}, u32[]{:S(2)}, u32[]{:S(2)}) collective-permute-start(bf16[1,1024,1024]{2,1,0:T(8,128)(2,1)} %get-tuple-element.38.rest_3_), channel_id=1, source_target_pairs={{0,1},{1,0},{2,3},{3,2},{4,5},{5,4},{6,7},{7,6},{8,9},{9,8},{10,11... | collective-permute-start | bytes 6291464 | tf_op jit(solution)/shard_map/ppermute | solution.py:133
  69.9 126.2 %collective-permute-start.14 = (bf16[4,1024]{1,0:T(4,128)(2,1)S(1)}, bf16[4,1024]{1,0:T(4,128)(2,1)S(1)}, u32[]{:S(2)}, u32[]{:S(2)}) collective-permute-start(bf16[4,1024]{1,0:T(4,128)(2,1)S(1)} %fusion), channel_id=1, source_target_pairs={{0,1},{1,0},{2,3},{3,2},{4,5},{5,4},{6,7},{7,6},{8,9},{9,8},{10,11... | collective-permute-start | bytes 24584 | tf_op jit(solution)/shard_map/ppermute | solution.py:133
  196.2 48.8 %collective-permute-start.2 = (bf16[1,1024,1024]{2,1,0:T(8,128)(2,1)}, bf16[1,1024,1024]{2,1,0:T(8,128)(2,1)}, u32[]{:S(2)}, u32[]{:S(2)}) collective-permute-start(bf16[1,1024,1024]{2,1,0:T(8,128)(2,1)} %get-tuple-element.39.rest_2_), channel_id=1, source_target_pairs={{0,1},{1,0},{2,3},{3,2},{4,5},{5,4},{6,7},{7,6},{8,9},{9,8},{10,11... | collective-permute-start | bytes 6291464 | tf_op jit(solution)/shard_map/ppermute | solution.py:133
  208.3 81.7 %collective-permute-start.13 = (bf16[1,1024,1024]{2,1,0:T(8,128)(2,1)}, bf16[1,1024,1024]{2,1,0:T(8,128)(2,1)}, u32[]{:S(2)}, u32[]{:S(2)}) collective-permute-start(bf16[1,1024,1024]{2,1,0:T(8,128)(2,1)} %get-tuple-element.42.rest_3_), channel_id=1, source_target_pairs={{0,1},{1,0},{2,3},{3,2},{4,5},{5,4},{6,7},{7,6},{8,9},{9,8},{10,11... | collective-permute-start | bytes 6291464 | tf_op jit(solution)/shard_map/ppermute | solution.py:133
  210.1 124.8 %collective-permute-start.12 = (bf16[1,1024,1024]{2,1,0:T(8,128)(2,1)}, bf16[1,1024,1024]{2,1,0:T(8,128)(2,1)}, u32[]{:S(2)}, u32[]{:S(2)}) collective-permute-start(bf16[1,1024,1024]{2,1,0:T(8,128)(2,1)} %get-tuple-element.44.rest_3_), channel_id=1, source_target_pairs={{0,1},{1,0},{2,3},{3,2},{4,5},{5,4},{6,7},{7,6},{8,9},{9,8},{10,11... | collective-permute-start | bytes 6291464 | tf_op jit(solution)/shard_map/ppermute | solution.py:133
  210.4 7.7 %copy-start.11 = (f32[1,1,1024]{2,1,0:T(1,128)S(1)}, f32[1,1,1024]{2,1,0:T(1,128)}, u32[]{:S(2)}) copy-start(f32[1,1,1024]{2,1,0:T(1,128)} %shard_map.110.rest_0_) | copy-start | bytes 12292
  210.4 7.7 %copy-start.14 = (f32[1,1,1024]{2,1,0:T(1,128)S(1)}, f32[1,1,1024]{2,1,0:T(1,128)}, u32[]{:S(2)}) copy-start(f32[1,1,1024]{2,1,0:T(1,128)} %copy-done.13) | copy-start | bytes 12292
  216.3 5.2 %copy-start.4 = (bf16[1,1024,1024]{2,1,0:T(8,128)(2,1)}, bf16[1,1024,1024]{2,1,0:T(8,128)(2,1)S(1)}, u32[]{:S(2)}) copy-start(bf16[1,1024,1024]{2,1,0:T(8,128)(2,1)S(1)} %collective-permute-done.4.piece_ref) | copy-start | bytes 6291460
  216.3 163.5 %collective-permute-start.11 = (bf16[1,1024,1024]{2,1,0:T(8,128)(2,1)}, bf16[1,1024,1024]{2,1,0:T(8,128)(2,1)}, u32[]{:S(2)}, u32[]{:S(2)}) collective-permute-start(bf16[1,1024,1024]{2,1,0:T(8,128)(2,1)} %get-tuple-element.46.rest_3_), channel_id=1, source_target_pairs={{0,1},{1,0},{2,3},{3,2},{4,5},{5,4},{6,7},{7,6},{8,9},{9,8},{10,11... | collective-permute-start | bytes 6291464 | tf_op jit(solution)/shard_map/ppermute | solution.py:133
  221.5 180.7 %collective-permute-start.10 = (bf16[1,512,1024]{2,1,0:T(8,128)(2,1)}, bf16[1,512,1024]{2,1,0:T(8,128)(2,1)S(1)}, u32[]{:S(2)}, u32[]{:S(2)}) collective-permute-start(bf16[1,512,1024]{2,1,0:T(8,128)(2,1)} %get-tuple-element.48.rest_3_), channel_id=1, source_target_pairs={{0,1},{1,0},{2,3},{3,2},{4,5},{5,4},{6,7},{7,6},{8,9},{9,8},{10,11... | collective-permute-start | bytes 3145736 | tf_op jit(solution)/shard_map/ppermute | solution.py:133
  227.0 2.2 copy-start
  227.0 2.2 copy-start.3
  227.0 18.0 %copy-start.6 = (bf16[1,256,1024]{2,1,0:T(8,128)(2,1)S(1)}, bf16[1,256,1024]{2,1,0:T(8,128)(2,1)}, u32[]{:S(2)}) copy-start(bf16[1,256,1024]{2,1,0:T(8,128)(2,1)} %get-tuple-element.50.rest_3_) | copy-start | bytes 1572868
  227.0 62.9 %copy-start.8 = (bf16[1,128,1024]{2,1,0:T(8,128)(2,1)S(1)}, bf16[1,128,1024]{2,1,0:T(8,128)(2,1)}, u32[]{:S(2)}) copy-start(bf16[1,128,1024]{2,1,0:T(8,128)(2,1)} %get-tuple-element.52.rest_3_) | copy-start | bytes 786436
  245.0 168.4 %collective-permute-start.9 = (bf16[1,256,1024]{2,1,0:T(8,128)(2,1)S(1)}, bf16[1,256,1024]{2,1,0:T(8,128)(2,1)S(1)}, u32[]{:S(2)}, u32[]{:S(2)}) collective-permute-start(bf16[1,256,1024]{2,1,0:T(8,128)(2,1)S(1)} %copy-done.6), channel_id=1, source_target_pairs={{0,1},{1,0},{2,3},{3,2},{4,5},{5,4},{6,7},{7,6},{8,9},{9,8},{10,11... | collective-permute-start | bytes 1572872 | tf_op jit(solution)/shard_map/ppermute | solution.py:133
  289.9 128.6 %collective-permute-start.8 = (bf16[1,128,1024]{2,1,0:T(8,128)(2,1)S(1)}, bf16[1,128,1024]{2,1,0:T(8,128)(2,1)S(1)}, u32[]{:S(2)}, u32[]{:S(2)}) collective-permute-start(bf16[1,128,1024]{2,1,0:T(8,128)(2,1)S(1)} %copy-done.8), channel_id=1, source_target_pairs={{0,1},{1,0},{2,3},{3,2},{4,5},{5,4},{6,7},{7,6},{8,9},{9,8},{10,11... | collective-permute-start | bytes 786440 | tf_op jit(solution)/shard_map/ppermute | solution.py:133
  334.9 86.4 %collective-permute-start.7 = (bf16[1,128,1024]{2,1,0:T(8,128)(2,1)}, bf16[1,128,1024]{2,1,0:T(8,128)(2,1)S(1)}, u32[]{:S(2)}, u32[]{:S(2)}) collective-permute-start(bf16[1,128,1024]{2,1,0:T(8,128)(2,1)} %get-tuple-element.53.rest_1_), channel_id=1, source_target_pairs={{0,1},{1,0},{2,3},{3,2},{4,5},{5,4},{6,7},{7,6},{8,9},{9,8},{10,11... | collective-permute-start | bytes 786440 | tf_op jit(solution)/shard_map/ppermute | solution.py:133
  402.2 1.0 copy-start.5
  413.4 0.8 copy-start.7
  418.5 0.7 copy-start.9
  421.3 0.7 copy-start.10
